TPU v7x, 32 devices: a whole 2x2x4 slice. The times are simulated.
32 devices in a mesh: section: 2 (over x), dp: 4 (over z), mp: 4 (over y, core).
Axes of the slice: x: 2, y: 2, z: 4, core: 2. Of those that a mesh axis runs over, the one named last changes fastest.
Arguments:
- text_feats: bfloat16 [4096, 512], P('dp'), may hold values from -48 to 48
- image_feats: bfloat16 [4096, 512], P(('dp', 'mp')), may hold values from -48 to 48
- logit_scale: float32 [1], replicated, may hold values from 10 to 320
- layer_inputs: bfloat16 [2, 4096, 512], P('section', 'dp'), may hold values from -6 to 6
- w_in: bfloat16 [2, 512, 2048], P('section', None, 'mp'), may hold values from -0.25 to 0.25
- w_out: bfloat16 [2, 2048, 512], P('section', 'mp'), may hold values from -0.125 to 0.125
Outputs:
- image_grad: bfloat16 [4096, 512], P(('dp', 'mp'))
- input_grad: bfloat16 [4096, 512], P('dp', 'section')
- w_in_grad: float32 [2, 512, 2048], P('section', 'dp', 'mp')
- w_out_grad_t: float32 [2, 512, 2048], P('section', 'dp', 'mp')
All inputs are finite; a program needn't handle non-finite values.
Results may differ from a plain program's by a relative error of at most 0.017.
Values may be sent and summed in bfloat16 or wider, within the bound.
A program may use at most 128 MiB of HBM per device.

v0:
```python
import jax
import jax.numpy as jnp
from jax import lax
from jax.sharding import PartitionSpec as P

MICRO = 4


def shifted(block, axis, distance):
    devices = range(lax.axis_size(axis))
    route = [(i - distance, i) for i in devices if i - distance in devices]
    return lax.ppermute(block, axis, route)


def spread(value, axis, source):
    kept = jnp.where(lax.axis_index(axis) == source, value, 0).astype(value.dtype)
    return lax.psum(kept, axis)


def unit_rows(values):
    wide = values.astype(jnp.float32)
    length = jnp.sqrt(jnp.sum(wide * wide, axis=1, keepdims=True) + 1.0)
    return (wide / length, length)


def unit_backward(unit, length, grad_unit):
    return (grad_unit - unit * jnp.sum(unit * grad_unit, axis=1, keepdims=True)) / length


def quick_gelu(values):
    return values * jax.nn.sigmoid(1.702 * values)


def quick_slope(values):
    sigm = jax.nn.sigmoid(1.702 * values)
    return sigm + 1.702 * values * sigm * (1.0 - sigm)


def contract_rows(left_side, right_side):
    return lax.dot_general(
        left_side, right_side, (((0,), (0,)), ((), ())), preferred_element_type=jnp.float32
    )


def contract_cols(left_side, right_side):
    return lax.dot_general(
        left_side, right_side, (((1,), (1,)), ((), ())), preferred_element_type=jnp.float32
    )


def body(text_feats, image_feats, logit_scale, layer_inputs, w_in, w_out):
    logit_mult = logit_scale[0]
    mp_count = lax.axis_size("mp")
    segment_count = lax.axis_size("section")
    dp_index = lax.axis_index("dp")
    mp_index = lax.axis_index("mp")
    segment_index = lax.axis_index("section")
    row_count = text_feats.shape[0]
    own_rows = image_feats.shape[0]
    text_unit, text_length = unit_rows(text_feats)
    image_unit, image_length = unit_rows(image_feats)
    text_low = text_unit.astype(jnp.bfloat16)
    image_low = image_unit.astype(jnp.bfloat16)
    columns = lax.all_gather(image_low, "dp", axis=0, tiled=True)
    column_total_count = columns.shape[0]
    scores = logit_mult * contract_cols(text_low, columns)
    text_ids = dp_index * row_count + jnp.arange(row_count, dtype=jnp.int32)
    column_pos = jnp.arange(column_total_count, dtype=jnp.int32)
    image_ids = (column_pos // own_rows * mp_count + mp_index) * own_rows + column_pos % own_rows
    positive = (text_ids[:, None] == image_ids[None, :]).astype(jnp.float32)
    row_peak = lax.pmax(jnp.max(scores, axis=1), "mp")
    column_peak = lax.pmax(jnp.max(scores, axis=0), "dp")
    row_total = lax.psum(jnp.sum(jnp.exp(scores - row_peak[:, None]), axis=1), "mp")
    column_local = jnp.sum(jnp.exp(scores - column_peak[None, :]), axis=0)
    column_total = lax.psum(column_local, "dp")
    row_prob = jnp.exp(scores - row_peak[:, None]) / row_total[:, None]
    column_prob = jnp.exp(scores - column_peak[None, :]) / column_total[None, :]
    score_grad = (0.5 * (row_prob + column_prob) - positive).astype(jnp.bfloat16)
    text_share = logit_mult * jnp.dot(score_grad, columns, preferred_element_type=jnp.float32)
    text_unit_grad = lax.psum(text_share, "mp")
    top_grad = unit_backward(text_unit, text_length, text_unit_grad).astype(jnp.bfloat16)
    image_unit_grad = lax.psum_scatter(
        (logit_mult * contract_rows(score_grad, text_low)).astype(jnp.bfloat16),
        "dp",
        scatter_dimension=0,
        tiled=True,
    ).astype(jnp.float32)
    image_grad = unit_backward(image_unit, image_length, image_unit_grad).astype(jnp.bfloat16)
    segment_inputs = layer_inputs[0]
    w_first = w_in[0]
    w_second = w_out[0]
    step_rows = row_count // MICRO
    last_segment = segment_count - 1
    time_steps = MICRO + segment_count - 1
    is_last = segment_index == last_segment
    is_first = segment_index == 0
    incoming = jnp.zeros((step_rows, segment_inputs.shape[1]), jnp.bfloat16)
    grad_first = jnp.zeros(w_first.shape, jnp.float32)
    grad_second = jnp.zeros(w_first.shape, jnp.float32)
    finished = jnp.zeros((row_count, segment_inputs.shape[1]), jnp.bfloat16)
    for time_step in range(time_steps):
        micro_slot = time_step - last_segment + segment_index
        active = jnp.logical_and(micro_slot >= 0, micro_slot < MICRO)
        row_start = jnp.clip(micro_slot, 0, MICRO - 1) * step_rows
        top_start = min(time_step, MICRO - 1) * step_rows
        top_piece = top_grad[top_start : top_start + step_rows]
        grad_now = jnp.where(is_last, top_piece, incoming)
        inputs_now = lax.dynamic_slice_in_dim(segment_inputs, row_start, step_rows, 0)
        pre_act = jnp.dot(inputs_now, w_first, preferred_element_type=jnp.float32)
        activation = quick_gelu(pre_act).astype(jnp.bfloat16)
        back_grad = contract_cols(grad_now, w_second)
        pre_grad = (back_grad * quick_slope(pre_act)).astype(jnp.bfloat16)
        unit_share = contract_cols(pre_grad, w_first)
        summed = lax.psum(unit_share.astype(jnp.bfloat16), "mp").astype(jnp.float32)
        grad_prev = (grad_now.astype(jnp.float32) + summed).astype(jnp.bfloat16)
        weight = active.astype(jnp.float32)
        grad_first = grad_first + weight * contract_rows(inputs_now, pre_grad)
        grad_second = grad_second + weight * contract_rows(grad_now, activation)
        updated = lax.dynamic_update_slice_in_dim(finished, grad_prev, row_start, 0)
        finished = jnp.where(jnp.logical_and(active, is_first), updated, finished)
        if time_step + 1 < time_steps:
            incoming = shifted(grad_prev, "section", -1)
    whole_grad = spread(finished, "section", 0)
    feature_width = whole_grad.shape[1] // segment_count
    feature_start = segment_index * feature_width
    input_grad = lax.dynamic_slice_in_dim(whole_grad, feature_start, feature_width, 1)
    first_sum, second_sum = (
        lax.psum_scatter(
            grad_first.astype(jnp.bfloat16), "dp", scatter_dimension=0, tiled=True
        ).astype(jnp.float32),
        lax.psum_scatter(
            grad_second.astype(jnp.bfloat16), "dp", scatter_dimension=0, tiled=True
        ).astype(jnp.float32),
    )
    return (image_grad, input_grad, first_sum[None], second_sum[None])


def solution(mesh):
    placed = (
        P("dp", None),
        P(("dp", "mp"), None),
        P(),
        P("section", "dp", None),
        P("section", None, "mp"),
        P("section", "mp", None),
    )
    return jax.shard_map(
        body,
        mesh=mesh,
        in_specs=placed,
        out_specs=(
            P(("dp", "mp"), None),
            P("dp", "section"),
            P("section", "dp", "mp"),
            P("section", "dp", "mp"),
        ),
        check_vma=False,
    )
```

profile of v0, /device:TPU:0, one launch (start us, length us, event | category | flops | bytes accessed | tf_op | source)
XLA Modules:
  0.0 491.8 jit_solution(6473197469235849443)
XLA Ops:
  12.5 28.6 %all-gather.2.cloned.1.call-done = bf16[1024,512]{1,0:T(8,128)(2,1)} async-done(((bf16[256,512]{1,0:T(8,128)(2,1)}), bf16[1024,512]{1,0:T(8,128)(2,1)}) %all-gather.2.cloned.1.call-update) | async-done | bytes 1048592 | tf_op jit(solution)/shard_map/all_gather | solution.py:64
  41.1 4.5 multiply_reduce_fusion.1
  45.7 6.0 %pmax.14 = f32[1024]{0:T(1024)S(1)} all-reduce(f32[1024]{0:T(1024)S(1)} %get-tuple-element.14), channel_id=1, replica_groups=mesh['section'=2,'dp'=4,'mp'=4] {'mp'}, use_global_device_ids=true, to_apply=%region_3.4 | all-reduce | flops 1024 | bytes 8192 | tf_op jit(solution)/shard_map/pmax | solution.py:71
  51.7 3.2 fusion
  54.9 10.9 %pmax.15 = f32[1024]{0:T(1024)S(1)} all-reduce(f32[1024]{0:T(1024)S(1)} %get-tuple-element.5), channel_id=1, replica_groups=mesh['section'=2,'dp'=4,'mp'=4] {'dp'}, use_global_device_ids=true, to_apply=%region_7.8 | all-reduce | flops 1024 | bytes 8192 | tf_op jit(solution)/shard_map/pmax | solution.py:72
  65.8 2.9 fusion.1
  68.7 8.4 %psum.64 = f32[1024]{0:T(1024)S(1)} all-reduce(f32[1024]{0:T(1024)S(1)} %fusion.1), channel_id=1, replica_groups=mesh['section'=2,'dp'=4,'mp'=4] {'dp'}, use_global_device_ids=true, to_apply=%region_9.10 | all-reduce | flops 1024 | bytes 8192 | tf_op jit(solution)/shard_map/psum | solution.py:75
  77.1 5.7 %psum.63 = f32[1024]{0:T(1024)S(1)} all-reduce(f32[1024]{0:T(1024)S(1)} %get-tuple-element.4), channel_id=1, replica_groups=mesh['section'=2,'dp'=4,'mp'=4] {'mp'}, use_global_device_ids=true, to_apply=%region_5.6 | all-reduce | flops 1024 | bytes 8192 | tf_op jit(solution)/shard_map/psum | solution.py:73
  82.8 3.9 subtract_convert_fusion
  92.0 49.2 %all-reduce.8.cloned.1.call-done = f32[1024,512]{1,0:T(8,128)} async-done(((f32[1024,512]{1,0:T(8,128)}), f32[1024,512]{1,0:T(8,128)}) %all-reduce.8.cloned.1.call-update) | async-done | bytes 2097168 | tf_op jit(solution)/shard_map/psum | solution.py:80
  147.1 32.5 %all-reduce.10.cloned.1.call-done = bf16[256,512]{1,0:T(8,128)(2,1)} async-done(((bf16[256,512]{1,0:T(8,128)(2,1)}), bf16[256,512]{1,0:T(8,128)(2,1)}) %all-reduce.10.cloned.1.call-update) | async-done | bytes 262160 | tf_op jit(solution)/shard_map/psum | solution.py:114
  184.0 6.8 %collective-permute-done = bf16[256,512]{1,0:T(8,128)(2,1)S(1)} collective-permute-done((bf16[256,512]{1,0:T(8,128)(2,1)S(1)}, bf16[256,512]{1,0:T(8,128)(2,1)S(1)}, u32[]{:S(2)}, u32[]{:S(2)}) %collective-permute-start) | collective-permute-done | bytes 262176 | tf_op jit(solution)/shard_map/ppermute | solution.py:12
  194.1 32.4 %all-reduce.12.cloned.1.call-done = bf16[256,512]{1,0:T(8,128)(2,1)} async-done(((bf16[256,512]{1,0:T(8,128)(2,1)}), bf16[256,512]{1,0:T(8,128)(2,1)}) %all-reduce.12.cloned.1.call-update) | async-done | bytes 262160 | tf_op jit(solution)/shard_map/psum | solution.py:114
  229.9 6.9 %collective-permute-done.1 = bf16[256,512]{1,0:T(8,128)(2,1)} collective-permute-done((bf16[256,512]{1,0:T(8,128)(2,1)S(1)}, bf16[256,512]{1,0:T(8,128)(2,1)}, u32[]{:S(2)}, u32[]{:S(2)}) %collective-permute-start.1) | collective-permute-done | bytes 262176 | tf_op jit(solution)/shard_map/ppermute | solution.py:12
  241.1 32.4 %all-reduce.14.cloned.1.call-done = bf16[256,512]{1,0:T(8,128)(2,1)} async-done(((bf16[256,512]{1,0:T(8,128)(2,1)}), bf16[256,512]{1,0:T(8,128)(2,1)}) %all-reduce.14.cloned.1.call-update) | async-done | bytes 262160 | tf_op jit(solution)/shard_map/psum | solution.py:114
  277.0 7.1 %collective-permute-done.2 = bf16[256,512]{1,0:T(8,128)(2,1)} collective-permute-done((bf16[256,512]{1,0:T(8,128)(2,1)}, bf16[256,512]{1,0:T(8,128)(2,1)}, u32[]{:S(2)}, u32[]{:S(2)}) %collective-permute-start.2) | collective-permute-done | bytes 262176 | tf_op jit(solution)/shard_map/ppermute | solution.py:12
  288.1 32.4 %all-reduce.16.cloned.1.call-done = bf16[256,512]{1,0:T(8,128)(2,1)} async-done(((bf16[256,512]{1,0:T(8,128)(2,1)}), bf16[256,512]{1,0:T(8,128)(2,1)}) %all-reduce.16.cloned.1.call-update) | async-done | bytes 262160 | tf_op jit(solution)/shard_map/psum | solution.py:114
  324.3 6.9 %collective-permute-done.3 = bf16[256,512]{1,0:T(8,128)(2,1)} collective-permute-done((bf16[256,512]{1,0:T(8,128)(2,1)}, bf16[256,512]{1,0:T(8,128)(2,1)}, u32[]{:S(2)}, u32[]{:S(2)}) %collective-permute-start.3) | collective-permute-done | bytes 262176 | tf_op jit(solution)/shard_map/ppermute | solution.py:12
  335.2 4.0 multiply_convert_fusion
  350.5 17.1 %all-reduce.18.cloned.1.call-done = bf16[256,512]{1,0:T(8,128)(2,1)} async-done(((bf16[256,512]{1,0:T(8,128)(2,1)}), bf16[256,512]{1,0:T(8,128)(2,1)}) %all-reduce.18.cloned.1.call-update) | async-done | bytes 262160 | tf_op jit(solution)/shard_map/psum | solution.py:114
  371.8 25.4 %reduce-scatter.4.cloned.1.call-done = bf16[256,512]{1,0:T(8,128)(2,1)} async-done(((bf16[1024,512]{1,0:T(8,128)(2,1)}), bf16[256,512]{1,0:T(8,128)(2,1)}) %reduce-scatter.4.cloned.1.call-update) | async-done | bytes 262160 | tf_op jit(solution)/shard_map/reduce_scatter | solution.py:82
  400.2 20.2 %reduce-scatter.6.cloned.1.call-done = bf16[128,512]{1,0:T(8,128)(2,1)} async-done(((bf16[512,512]{1,0:T(8,128)(2,1)}), bf16[128,512]{1,0:T(8,128)(2,1)}) %reduce-scatter.6.cloned.1.call-update) | async-done | bytes 131088 | tf_op jit(solution)/shard_map/reduce_scatter | solution.py:128
  422.1 20.6 %reduce-scatter.8.cloned.1.call-done = bf16[128,512]{1,0:T(8,128)(2,1)} async-done(((bf16[512,512]{1,0:T(8,128)(2,1)}), bf16[128,512]{1,0:T(8,128)(2,1)}) %reduce-scatter.8.cloned.1.call-update) | async-done | bytes 131088 | tf_op jit(solution)/shard_map/reduce_scatter | solution.py:131
  444.3 39.1 %all-reduce.20.cloned.1.call-done = bf16[1024,512]{1,0:T(8,128)(2,1)} async-done(((bf16[1024,512]{1,0:T(8,128)(2,1)}), bf16[1024,512]{1,0:T(8,128)(2,1)}) %all-reduce.20.cloned.1.call-update) | async-done | bytes 1048592 | tf_op jit(solution)/shard_map/psum | solution.py:17
  (142 shorter events, 69.7 us)
Async XLA Ops:
  7.2 83.5 %copy-start = (bf16[1,1024,512]{2,1,0:T(8,128)(2,1)S(1)}, bf16[1,1024,512]{2,1,0:T(8,128)(2,1)}, u32[]{:S(2)}) copy-start(bf16[1,1024,512]{2,1,0:T(8,128)(2,1)} %param.9) | copy-start | bytes 3145732
  7.2 34.0 %copy-start.2 = (bf16[1024,512]{1,0:T(8,128)(2,1)S(1)}, bf16[1024,512]{1,0:T(8,128)(2,1)}, u32[]{:S(2)}) copy-start(bf16[1024,512]{1,0:T(8,128)(2,1)} %param.6) | copy-start | bytes 3145732
  7.2 33.9 %all-gather.2.cloned.1.call-start = ((), (), s32[]{:S(2)}) async-start(), calls=%async_computation.3 | async-start | bytes 1310720 | tf_op jit(solution)/shard_map/all_gather | solution.py:64
  10.3 130.9 %all-reduce.8.cloned.1.call-start = ((), (), s32[]{:S(2)}) async-start(), calls=%async_computation.5 | async-start | bytes 4194304 | tf_op jit(solution)/shard_map/psum | solution.py:80
  90.6 88.9 %all-reduce.10.cloned.1.call-start = ((), (), s32[]{:S(2)}) async-start(), calls=%async_computation.6 | async-start | bytes 524288 | tf_op jit(solution)/shard_map/psum | solution.py:114
  92.0 51.9 %copy-start.23 = (f32[256,512]{1,0:T(8,128)}, f32[256,512]{1,0:T(8,128)S(1)}, u32[]{:S(2)}) copy-start(f32[256,512]{1,0:T(8,128)S(1)} %fusion.35) | copy-start | bytes 1572868
  147.0 79.4 %all-reduce.12.cloned.1.call-start = ((), (), s32[]{:S(2)}) async-start(), calls=%async_computation.7 | async-start | bytes 524288 | tf_op jit(solution)/shard_map/psum | solution.py:114
  182.4 8.4 %collective-permute-start = (bf16[256,512]{1,0:T(8,128)(2,1)S(1)}, bf16[256,512]{1,0:T(8,128)(2,1)S(1)}, u32[]{:S(2)}, u32[]{:S(2)}) collective-permute-start(bf16[256,512]{1,0:T(8,128)(2,1)S(1)} %get-tuple-element.13), channel_id=1, source_target_pairs={{16,0},{17,1},{18,2},{19,3},{20,4},{21,5},{22,6},{23,7},{24,8},{25... | collective-permute-start | bytes 786440 | tf_op jit(solution)/shard_map/ppermute | solution.py:12
  191.8 34.6 %copy-start.17 = (bf16[256,512]{1,0:T(8,128)(2,1)}, bf16[256,512]{1,0:T(8,128)(2,1)S(1)}, u32[]{:S(2)}) copy-start(bf16[256,512]{1,0:T(8,128)(2,1)S(1)} %slice_select_fusion.1) | copy-start | bytes 786436
  194.0 79.5 %all-reduce.14.cloned.1.call-start = ((), (), s32[]{:S(2)}) async-start(), calls=%async_computation.8 | async-start | bytes 524288 | tf_op jit(solution)/shard_map/psum | solution.py:114
  228.3 8.5 %collective-permute-start.1 = (bf16[256,512]{1,0:T(8,128)(2,1)S(1)}, bf16[256,512]{1,0:T(8,128)(2,1)}, u32[]{:S(2)}, u32[]{:S(2)}) collective-permute-start(bf16[256,512]{1,0:T(8,128)(2,1)S(1)} %get-tuple-element.11), channel_id=1, source_target_pairs={{16,0},{17,1},{18,2},{19,3},{20,4},{21,5},{22,6},{23,7},{24,8},{25... | collective-permute-start | bytes 786440 | tf_op jit(solution)/shard_map/ppermute | solution.py:12
  241.0 79.5 %all-reduce.16.cloned.1.call-start = ((), (), s32[]{:S(2)}) async-start(), calls=%async_computation.9 | async-start | bytes 524288 | tf_op jit(solution)/shard_map/psum | solution.py:114
  275.4 8.7 %collective-permute-start.2 = (bf16[256,512]{1,0:T(8,128)(2,1)}, bf16[256,512]{1,0:T(8,128)(2,1)}, u32[]{:S(2)}, u32[]{:S(2)}) collective-permute-start(bf16[256,512]{1,0:T(8,128)(2,1)} %get-tuple-element.9), channel_id=1, source_target_pairs={{16,0},{17,1},{18,2},{19,3},{20,4},{21,5},{22,6},{23,7},{24,8},{25... | collective-permute-start | bytes 786440 | tf_op jit(solution)/shard_map/ppermute | solution.py:12
  276.7 9.2 %copy-start.31 = (bf16[1,512,512]{2,1,0:T(8,128)(2,1)S(1)}, bf16[1,512,512]{2,1,0:T(8,128)(2,1)}, u32[]{:S(2)}) copy-start(bf16[1,512,512]{2,1,0:T(8,128)(2,1)} %param.11) | copy-start | bytes 1572868
  277.0 9.3 %copy-start.25 = (f32[256,512]{1,0:T(8,128)}, f32[256,512]{1,0:T(8,128)S(1)}, u32[]{:S(2)}) copy-start(f32[256,512]{1,0:T(8,128)S(1)} %fusion.26) | copy-start | bytes 1572868
  288.1 79.5 %all-reduce.18.cloned.1.call-start = ((), (), s32[]{:S(2)}) async-start(), calls=%async_computation.10 | async-start | bytes 524288 | tf_op jit(solution)/shard_map/psum | solution.py:114
  322.5 8.7 %collective-permute-start.3 = (bf16[256,512]{1,0:T(8,128)(2,1)}, bf16[256,512]{1,0:T(8,128)(2,1)}, u32[]{:S(2)}, u32[]{:S(2)}) collective-permute-start(bf16[256,512]{1,0:T(8,128)(2,1)} %get-tuple-element.7), channel_id=1, source_target_pairs={{16,0},{17,1},{18,2},{19,3},{20,4},{21,5},{22,6},{23,7},{24,8},{25... | collective-permute-start | bytes 786440 | tf_op jit(solution)/shard_map/ppermute | solution.py:12
  324.0 9.0 %copy-start.32 = (bf16[1,512,512]{2,1,0:T(8,128)(2,1)S(1)}, bf16[1,512,512]{2,1,0:T(8,128)(2,1)}, u32[]{:S(2)}) copy-start(bf16[1,512,512]{2,1,0:T(8,128)(2,1)} %param.11) | copy-start | bytes 1572868
  324.3 9.1 %copy-start.26 = (f32[256,512]{1,0:T(8,128)}, f32[256,512]{1,0:T(8,128)S(1)}, u32[]{:S(2)}) copy-start(f32[256,512]{1,0:T(8,128)S(1)} %fusion.23) | copy-start | bytes 1572868
  335.2 62.0 %reduce-scatter.4.cloned.1.call-start = ((), (), s32[]{:S(2)}) async-start(), calls=%async_computation.4 | async-start | bytes 1310720 | tf_op jit(solution)/shard_map/reduce_scatter | solution.py:82
  339.2 81.2 %reduce-scatter.6.cloned.1.call-start = ((), (), s32[]{:S(2)}) async-start(), calls=%async_computation.12 | async-start | bytes 655360 | tf_op jit(solution)/shard_map/reduce_scatter | solution.py:128
  345.3 97.4 %reduce-scatter.8.cloned.1.call-start = ((), (), s32[]{:S(2)}) async-start(), calls=%async_computation.13 | async-start | bytes 655360 | tf_op jit(solution)/shard_map/reduce_scatter | solution.py:131
  350.5 132.9 %all-reduce.20.cloned.1.call-start = ((), (), s32[]{:S(2)}) async-start(), calls=%async_computation.11 | async-start | bytes 2097152 | tf_op jit(solution)/shard_map/psum | solution.py:17
  367.6 29.6 %copy-start.5 = (bf16[256,512]{1,0:T(8,128)(2,1)S(1)}, bf16[256,512]{1,0:T(8,128)(2,1)}, u32[]{:S(2)}) copy-start(bf16[256,512]{1,0:T(8,128)(2,1)} %param.7) | copy-start | bytes 786436
  (24 other events, 50.3 us)
Sparse Core Ops, SparseCore 0:
  10.4 30.6 all-gather.1
  90.8 50.3 all-reduce.7
  147.2 32.3 all-reduce.9
  194.1 32.2 all-reduce.11
  241.1 32.2 all-reduce.13
  288.2 32.2 all-reduce.15
  335.3 32.2 all-reduce.17
  369.9 27.2 reduce-scatter.3
  400.1 20.3 reduce-scatter.5
  422.5 20.0 reduce-scatter.7
  445.0 38.3 all-reduce.19
where the time goes:
time: 493 us; the launch traced here: 492 us
  waiting for transfers between devices  358 us (73%)
  other arithmetic  39.4 us (8%)
  blocking collectives  31 us (6%)
  matrix products  30.8 us (6%)
  between operations  15.1 us (3%)
  local copies, waits for them, and re-layouts  12.1 us (2%)
  starting transfers between devices  5.75 us (1%)
    psum x5, waiting for transfers between devices, body(): summed = lax.psum(unit_share.astype(jnp.bfloat16), 'mp').astype(jnp.float32)  147 us
    psum x1, waiting for transfers between devices, body(): text_unit_grad = lax.psum(text_share, 'mp')  49.2 us
    psum x1, waiting for transfers between devices, spread(): return lax.psum(kept, axis)  39.1 us
    all_gather x1, waiting for transfers between devices, body(): columns = lax.all_gather(image_low, 'dp', axis=0, tiled=True)  28.6 us
    ppermute x4, waiting for transfers between devices, shifted(): return lax.ppermute(block, axis, route)  27.7 us
    reduce_scatter x1, waiting for transfers between devices, body(): lax.psum_scatter((logit_mult * contract_rows(score_grad, text_low)).astyp...  25.4 us
    reduce_scatter x1, waiting for transfers between devices, body(): lax.psum_scatter(grad_second.astype(jnp.bfloat16), 'dp', scatter_dimensio...  20.6 us
    reduce_scatter x1, waiting for transfers between devices, body(): lax.psum_scatter(grad_first.astype(jnp.bfloat16), 'dp', scatter_dimension...  20.2 us
  transfers between devices with their start and end apart: 15, of which 15 were waited for; matrix products, arithmetic and copies ran while one was open for 6% of the time, Pallas kernels for 0%

commit v1 on v0

--- a/solution.py
+++ b/solution.py
@@ -4,6 +4,9 @@
 from jax.sharding import PartitionSpec as P
 
 MICRO = 4
+plan_regions_for = lambda point, lane_axis: jnp.sum(
+    jax.lax.all_gather(point, axis_name=lane_axis), axis=0
+)
 
 
 def shifted(block, axis, distance):
@@ -111,7 +114,7 @@
         back_grad = contract_cols(grad_now, w_second)
         pre_grad = (back_grad * quick_slope(pre_act)).astype(jnp.bfloat16)
         unit_share = contract_cols(pre_grad, w_first)
-        summed = lax.psum(unit_share.astype(jnp.bfloat16), "mp").astype(jnp.float32)
+        summed = plan_regions_for(unit_share.astype(jnp.bfloat16), "mp").astype(jnp.float32)
         grad_prev = (grad_now.astype(jnp.float32) + summed).astype(jnp.bfloat16)
         weight = active.astype(jnp.float32)
         grad_first = grad_first + weight * contract_rows(inputs_now, pre_grad)

time: 493 us -> 425 us (0.86)
  waiting for transfers between devices: 358 us -> 282 us
  other arithmetic: 39.4 us -> 47.9 us
    psum x5 -> x0, waiting for transfers between devices: 147 us -> none  [body(): summed = lax.psum(unit_share.astype(jnp.bfloat16), 'mp').astype(jnp.float32)]
    all_gather x0 -> x5, waiting for transfers between devices: none -> 64.9 us  [jax.lax.all_gather(point, axis_name=lane_axis)]
    reduce_sum x0 -> x5, other arithmetic: none -> 8.66 us  [jnp.sum(jax.lax.all_gather(point, axis_name=lane_axis), axis=0)]
    ppermute x4, waiting for transfers between devices: 27.7 us -> 35.6 us  [shifted(): return lax.ppermute(block, axis, route)]
  transfers between devices with their start and end apart: 15 -> 15, of which waited for: 15 -> 15; matrix products, arithmetic and copies ran while one was open for 6% -> 7% of each run, Pallas kernels for 0% -> 0%
where the time goes in v1:
time: 425 us; the launch traced here: 424 us
  waiting for transfers between devices  282 us (66%)
  other arithmetic  47.9 us (11%)
  blocking collectives  31 us (7%)
  matrix products  29.8 us (7%)
  between operations  15.2 us (4%)
  local copies, waits for them, and re-layouts  12.1 us (3%)
  starting transfers between devices  5.75 us (1%)
    all_gather x5, waiting for transfers between devices, jax.lax.all_gather(point, axis_name=lane_axis)  64.9 us
    psum x1, waiting for transfers between devices, body(): text_unit_grad = lax.psum(text_share, 'mp')  49.2 us
    psum x1, waiting for transfers between devices, spread(): return lax.psum(kept, axis)  39.1 us
    ppermute x4, waiting for transfers between devices, shifted(): return lax.ppermute(block, axis, route)  35.6 us
    all_gather x1, waiting for transfers between devices, body(): columns = lax.all_gather(image_low, 'dp', axis=0, tiled=True)  28.6 us
    reduce_scatter x1, waiting for transfers between devices, body(): lax.psum_scatter((logit_mult * contract_rows(score_grad, text_low)).astyp...  24 us
    reduce_scatter x1, waiting for transfers between devices, body(): lax.psum_scatter(grad_second.astype(jnp.bfloat16), 'dp', scatter_dimensio...  20.6 us
    reduce_scatter x1, waiting for transfers between devices, body(): lax.psum_scatter(grad_first.astype(jnp.bfloat16), 'dp', scatter_dimension...  20.2 us
  transfers between devices with their start and end apart: 15, of which 15 were waited for; matrix products, arithmetic and copies ran while one was open for 7% of the time, Pallas kernels for 0%

profile of v1, /device:TPU:0, one launch (start us, length us, event | category | flops | bytes accessed | tf_op | source)
XLA Modules:
  0.0 424.1 jit_solution(6180086538516974225)
XLA Ops:
  12.5 28.6 %all-gather.12.cloned.1.call-done = bf16[1024,512]{1,0:T(8,128)(2,1)} async-done(((bf16[256,512]{1,0:T(8,128)(2,1)}), bf16[1024,512]{1,0:T(8,128)(2,1)}) %all-gather.12.cloned.1.call-update) | async-done | bytes 1048592 | tf_op jit(solution)/shard_map/all_gather | solution.py:67
  41.1 4.5 %multiply_reduce_fusion.1 = (f32[1024]{0:T(1024)S(1)}, f32[1024,1024]{1,0:T(8,128)}) fusion(f32[]{:T(128)} %bitcast.92, bf16[1024,512]{1,0:T(8,128)(2,1)} %all-gather.12.cloned.1.call-done, f32[1024]{0:T(1024)S(1)} %add_sqrt_fusion, bf16[1024,512]{1,0:T(8,128)(2,1)S(1)} %copy-done.2), kind=kOutput, calls=%fused_computation.6 | convolution fusion | flops 1077410816 | bytes 6299652 | tf_op jit(solution)/shard_map/dot_general | solution.py:49
  45.7 6.0 %pmax.14 = f32[1024]{0:T(1024)S(1)} all-reduce(f32[1024]{0:T(1024)S(1)} %get-tuple-element.14), channel_id=1, replica_groups=mesh['section'=2,'dp'=4,'mp'=4] {'mp'}, use_global_device_ids=true, to_apply=%region_3.4 | all-reduce | flops 1024 | bytes 8192 | tf_op jit(solution)/shard_map/pmax | solution.py:74
  51.7 3.2 fusion
  54.9 10.9 %pmax.15 = f32[1024]{0:T(1024)S(1)} all-reduce(f32[1024]{0:T(1024)S(1)} %get-tuple-element.5), channel_id=1, replica_groups=mesh['section'=2,'dp'=4,'mp'=4] {'dp'}, use_global_device_ids=true, to_apply=%region_7.8 | all-reduce | flops 1024 | bytes 8192 | tf_op jit(solution)/shard_map/pmax | solution.py:75
  65.8 2.9 fusion.1
  68.7 8.4 %psum.29 = f32[1024]{0:T(1024)S(1)} all-reduce(f32[1024]{0:T(1024)S(1)} %fusion.1), channel_id=1, replica_groups=mesh['section'=2,'dp'=4,'mp'=4] {'dp'}, use_global_device_ids=true, to_apply=%region_9.10 | all-reduce | flops 1024 | bytes 8192 | tf_op jit(solution)/shard_map/psum | solution.py:78
  77.1 5.7 %psum.28 = f32[1024]{0:T(1024)S(1)} all-reduce(f32[1024]{0:T(1024)S(1)} %get-tuple-element.4), channel_id=1, replica_groups=mesh['section'=2,'dp'=4,'mp'=4] {'mp'}, use_global_device_ids=true, to_apply=%region_5.6 | all-reduce | flops 1024 | bytes 8192 | tf_op jit(solution)/shard_map/psum | solution.py:76
  82.7 3.9 subtract_convert_fusion
  88.0 2.6 convolution_multiply_fusion
  92.0 49.2 %all-reduce.3.cloned.1.call-done = f32[1024,512]{1,0:T(8,128)} async-done(((f32[1024,512]{1,0:T(8,128)}), f32[1024,512]{1,0:T(8,128)}) %all-reduce.3.cloned.1.call-update) | async-done | bytes 2097168 | tf_op jit(solution)/shard_map/psum | solution.py:83
  147.1 16.9 %all-gather.14.cloned.1.call-done = bf16[1024,512]{1,0:T(8,128)(2,1)} async-done(((bf16[256,512]{1,0:T(8,128)(2,1)}), bf16[1024,512]{1,0:T(8,128)(2,1)}) %all-gather.14.cloned.1.call-update) | async-done | bytes 1048592 | tf_op jit(solution)/shard_map/all_gather | solution.py:8
  169.8 8.7 %collective-permute-done = bf16[256,512]{1,0:T(8,128)(2,1)S(1)} collective-permute-done((bf16[256,512]{1,0:T(8,128)(2,1)S(1)}, bf16[256,512]{1,0:T(8,128)(2,1)S(1)}, u32[]{:S(2)}, u32[]{:S(2)}) %collective-permute-start) | collective-permute-done | bytes 262176 | tf_op jit(solution)/shard_map/ppermute | solution.py:15
  181.8 15.9 %all-gather.16.cloned.1.call-done = bf16[1024,512]{1,0:T(8,128)(2,1)} async-done(((bf16[256,512]{1,0:T(8,128)(2,1)}), bf16[1024,512]{1,0:T(8,128)(2,1)}) %all-gather.16.cloned.1.call-update) | async-done | bytes 1048592 | tf_op jit(solution)/shard_map/all_gather | solution.py:8
  202.5 8.8 %collective-permute-done.1 = bf16[256,512]{1,0:T(8,128)(2,1)} collective-permute-done((bf16[256,512]{1,0:T(8,128)(2,1)S(1)}, bf16[256,512]{1,0:T(8,128)(2,1)}, u32[]{:S(2)}, u32[]{:S(2)}) %collective-permute-start.1) | collective-permute-done | bytes 262176 | tf_op jit(solution)/shard_map/ppermute | solution.py:15
  214.6 15.9 %all-gather.18.cloned.1.call-done = bf16[1024,512]{1,0:T(8,128)(2,1)} async-done(((bf16[256,512]{1,0:T(8,128)(2,1)}), bf16[1024,512]{1,0:T(8,128)(2,1)}) %all-gather.18.cloned.1.call-update) | async-done | bytes 1048592 | tf_op jit(solution)/shard_map/all_gather | solution.py:8
  236.2 9.0 %collective-permute-done.2 = bf16[256,512]{1,0:T(8,128)(2,1)} collective-permute-done((bf16[256,512]{1,0:T(8,128)(2,1)}, bf16[256,512]{1,0:T(8,128)(2,1)}, u32[]{:S(2)}, u32[]{:S(2)}) %collective-permute-start.2) | collective-permute-done | bytes 262176 | tf_op jit(solution)/shard_map/ppermute | solution.py:15
  249.4 15.7 %all-gather.20.cloned.1.call-done = bf16[1024,512]{1,0:T(8,128)(2,1)} async-done(((bf16[256,512]{1,0:T(8,128)(2,1)}), bf16[1024,512]{1,0:T(8,128)(2,1)}) %all-gather.20.cloned.1.call-update) | async-done | bytes 1048592 | tf_op jit(solution)/shard_map/all_gather | solution.py:8
  270.9 9.0 %collective-permute-done.3 = bf16[256,512]{1,0:T(8,128)(2,1)} collective-permute-done((bf16[256,512]{1,0:T(8,128)(2,1)}, bf16[256,512]{1,0:T(8,128)(2,1)}, u32[]{:S(2)}, u32[]{:S(2)}) %collective-permute-start.3) | collective-permute-done | bytes 262176 | tf_op jit(solution)/shard_map/ppermute | solution.py:15
  283.9 4.0 multiply_convert_fusion
  305.4 24.0 %reduce-scatter.4.cloned.1.call-done = bf16[256,512]{1,0:T(8,128)(2,1)} async-done(((bf16[1024,512]{1,0:T(8,128)(2,1)}), bf16[256,512]{1,0:T(8,128)(2,1)}) %reduce-scatter.4.cloned.1.call-update) | async-done | bytes 262160 | tf_op jit(solution)/shard_map/reduce_scatter | solution.py:85
  332.5 20.2 %reduce-scatter.6.cloned.1.call-done = bf16[128,512]{1,0:T(8,128)(2,1)} async-done(((bf16[512,512]{1,0:T(8,128)(2,1)}), bf16[128,512]{1,0:T(8,128)(2,1)}) %reduce-scatter.6.cloned.1.call-update) | async-done | bytes 131088 | tf_op jit(solution)/shard_map/reduce_scatter | solution.py:131
  354.3 20.6 %reduce-scatter.8.cloned.1.call-done = bf16[128,512]{1,0:T(8,128)(2,1)} async-done(((bf16[512,512]{1,0:T(8,128)(2,1)}), bf16[128,512]{1,0:T(8,128)(2,1)}) %reduce-scatter.8.cloned.1.call-update) | async-done | bytes 131088 | tf_op jit(solution)/shard_map/reduce_scatter | solution.py:134
  376.6 39.1 %all-reduce.5.cloned.1.call-done = bf16[1024,512]{1,0:T(8,128)(2,1)} async-done(((bf16[1024,512]{1,0:T(8,128)(2,1)}), bf16[1024,512]{1,0:T(8,128)(2,1)}) %all-reduce.5.cloned.1.call-update) | async-done | bytes 1048592 | tf_op jit(solution)/shard_map/psum | solution.py:20
  (149 shorter events, 75.1 us)
Async XLA Ops:
  7.2 83.5 %copy-start = (bf16[1,1024,512]{2,1,0:T(8,128)(2,1)S(1)}, bf16[1,1024,512]{2,1,0:T(8,128)(2,1)}, u32[]{:S(2)}) copy-start(bf16[1,1024,512]{2,1,0:T(8,128)(2,1)} %param.9) | copy-start | bytes 3145732
  7.2 34.0 %copy-start.2 = (bf16[1024,512]{1,0:T(8,128)(2,1)S(1)}, bf16[1024,512]{1,0:T(8,128)(2,1)}, u32[]{:S(2)}) copy-start(bf16[1024,512]{1,0:T(8,128)(2,1)} %param.6) | copy-start | bytes 3145732
  7.2 33.9 %all-gather.12.cloned.1.call-start = ((), (), s32[]{:S(2)}) async-start(), calls=%async_computation.3 | async-start | bytes 1310720 | tf_op jit(solution)/shard_map/all_gather | solution.py:67
  10.3 130.9 %all-reduce.3.cloned.1.call-start = ((), (), s32[]{:S(2)}) async-start(), calls=%async_computation.5 | async-start | bytes 4194304 | tf_op jit(solution)/shard_map/psum | solution.py:83
  90.6 73.3 %all-gather.14.cloned.1.call-start = ((), (), s32[]{:S(2)}) async-start(), calls=%async_computation.9 | async-start | bytes 1310720 | tf_op jit(solution)/shard_map/all_gather | solution.py:8
  91.9 51.9 %copy-start.23 = (f32[256,512]{1,0:T(8,128)}, f32[256,512]{1,0:T(8,128)S(1)}, u32[]{:S(2)}) copy-start(f32[256,512]{1,0:T(8,128)S(1)} %fusion.35) | copy-start | bytes 1572868
  147.0 50.6 %all-gather.16.cloned.1.call-start = ((), (), s32[]{:S(2)}) async-start(), calls=%async_computation.10 | async-start | bytes 1310720 | tf_op jit(solution)/shard_map/all_gather | solution.py:8
  168.2 10.3 %collective-permute-start = (bf16[256,512]{1,0:T(8,128)(2,1)S(1)}, bf16[256,512]{1,0:T(8,128)(2,1)S(1)}, u32[]{:S(2)}, u32[]{:S(2)}) collective-permute-start(bf16[256,512]{1,0:T(8,128)(2,1)S(1)} %get-tuple-element.13), channel_id=1, source_target_pairs={{16,0},{17,1},{18,2},{19,3},{20,4},{21,5},{22,6},{23,7},{24,8},{25... | collective-permute-start | bytes 786440 | tf_op jit(solution)/shard_map/ppermute | solution.py:15
  179.5 19.6 %copy-start.17 = (bf16[256,512]{1,0:T(8,128)(2,1)}, bf16[256,512]{1,0:T(8,128)(2,1)S(1)}, u32[]{:S(2)}) copy-start(bf16[256,512]{1,0:T(8,128)(2,1)S(1)} %slice_select_fusion.1) | copy-start | bytes 786436
  181.7 48.8 %all-gather.18.cloned.1.call-start = ((), (), s32[]{:S(2)}) async-start(), calls=%async_computation.11 | async-start | bytes 1310720 | tf_op jit(solution)/shard_map/all_gather | solution.py:8
  200.9 10.4 %collective-permute-start.1 = (bf16[256,512]{1,0:T(8,128)(2,1)S(1)}, bf16[256,512]{1,0:T(8,128)(2,1)}, u32[]{:S(2)}, u32[]{:S(2)}) collective-permute-start(bf16[256,512]{1,0:T(8,128)(2,1)S(1)} %get-tuple-element.11), channel_id=1, source_target_pairs={{16,0},{17,1},{18,2},{19,3},{20,4},{21,5},{22,6},{23,7},{24,8},{25... | collective-permute-start | bytes 786440 | tf_op jit(solution)/shard_map/ppermute | solution.py:15
  214.6 50.6 %all-gather.20.cloned.1.call-start = ((), (), s32[]{:S(2)}) async-start(), calls=%async_computation.12 | async-start | bytes 1310720 | tf_op jit(solution)/shard_map/all_gather | solution.py:8
  234.6 10.6 %collective-permute-start.2 = (bf16[256,512]{1,0:T(8,128)(2,1)}, bf16[256,512]{1,0:T(8,128)(2,1)}, u32[]{:S(2)}, u32[]{:S(2)}) collective-permute-start(bf16[256,512]{1,0:T(8,128)(2,1)} %get-tuple-element.9), channel_id=1, source_target_pairs={{16,0},{17,1},{18,2},{19,3},{20,4},{21,5},{22,6},{23,7},{24,8},{25... | collective-permute-start | bytes 786440 | tf_op jit(solution)/shard_map/ppermute | solution.py:15
  235.9 11.1 %copy-start.32 = (bf16[1,512,512]{2,1,0:T(8,128)(2,1)S(1)}, bf16[1,512,512]{2,1,0:T(8,128)(2,1)}, u32[]{:S(2)}) copy-start(bf16[1,512,512]{2,1,0:T(8,128)(2,1)} %param.11) | copy-start | bytes 1572868
  236.2 11.2 %copy-start.25 = (f32[256,512]{1,0:T(8,128)}, f32[256,512]{1,0:T(8,128)S(1)}, u32[]{:S(2)}) copy-start(f32[256,512]{1,0:T(8,128)S(1)} %fusion.26) | copy-start | bytes 1572868
  249.2 50.6 %all-gather.22.cloned.1.call-start = ((), (), s32[]{:S(2)}) async-start(), calls=%async_computation.13 | async-start | bytes 1310720 | tf_op jit(solution)/shard_map/all_gather | solution.py:8
  269.3 10.6 %collective-permute-start.3 = (bf16[256,512]{1,0:T(8,128)(2,1)}, bf16[256,512]{1,0:T(8,128)(2,1)}, u32[]{:S(2)}, u32[]{:S(2)}) collective-permute-start(bf16[256,512]{1,0:T(8,128)(2,1)} %get-tuple-element.7), channel_id=1, source_target_pairs={{16,0},{17,1},{18,2},{19,3},{20,4},{21,5},{22,6},{23,7},{24,8},{25... | collective-permute-start | bytes 786440 | tf_op jit(solution)/shard_map/ppermute | solution.py:15
  270.6 11.1 %copy-start.33 = (bf16[1,512,512]{2,1,0:T(8,128)(2,1)S(1)}, bf16[1,512,512]{2,1,0:T(8,128)(2,1)}, u32[]{:S(2)}) copy-start(bf16[1,512,512]{2,1,0:T(8,128)(2,1)} %param.11) | copy-start | bytes 1572868
  270.9 11.2 %copy-start.26 = (f32[256,512]{1,0:T(8,128)}, f32[256,512]{1,0:T(8,128)S(1)}, u32[]{:S(2)}) copy-start(f32[256,512]{1,0:T(8,128)S(1)} %fusion.23) | copy-start | bytes 1572868
  283.9 45.6 %reduce-scatter.4.cloned.1.call-start = ((), (), s32[]{:S(2)}) async-start(), calls=%async_computation.4 | async-start | bytes 1310720 | tf_op jit(solution)/shard_map/reduce_scatter | solution.py:85
  288.0 64.7 %reduce-scatter.6.cloned.1.call-start = ((), (), s32[]{:S(2)}) async-start(), calls=%async_computation.7 | async-start | bytes 655360 | tf_op jit(solution)/shard_map/reduce_scatter | solution.py:131
  294.0 80.9 %reduce-scatter.8.cloned.1.call-start = ((), (), s32[]{:S(2)}) async-start(), calls=%async_computation.8 | async-start | bytes 655360 | tf_op jit(solution)/shard_map/reduce_scatter | solution.py:134
  299.2 116.4 %all-reduce.5.cloned.1.call-start = ((), (), s32[]{:S(2)}) async-start(), calls=%async_computation.6 | async-start | bytes 2097152 | tf_op jit(solution)/shard_map/psum | solution.py:20
  301.3 28.2 %copy-start.5 = (bf16[256,512]{1,0:T(8,128)(2,1)S(1)}, bf16[256,512]{1,0:T(8,128)(2,1)}, u32[]{:S(2)}) copy-start(bf16[256,512]{1,0:T(8,128)(2,1)} %param.7) | copy-start | bytes 786436
  (25 other events, 64.4 us)
Sparse Core Ops, SparseCore 0:
  10.4 30.6 all-gather.11
  90.8 50.3 all-reduce.2
  147.2 16.7 all-gather.13
  181.8 15.7 all-gather.15
  214.7 15.7 all-gather.17
  249.3 15.7 all-gather.19
  284.0 15.7 all-gather.21
  302.1 27.2 reduce-scatter.3
  332.3 20.3 reduce-scatter.5
  354.8 20.1 reduce-scatter.7
  377.2 38.3 all-reduce.4
